TPU v7x, 32 devices: a whole 2x2x4 slice. The times are simulated.
32 devices in a mesh: row: 4 (over y, core), col: 8 (over z, x).
Axes of the slice: x: 2, y: 2, z: 4, core: 2. Of those that a mesh axis runs over, the one named last changes fastest.
Arguments:
- eigvecs: float32 [1024, 50176], P('col', 'row'), may hold values from -6 to 6
- span_vectors: float32 [2, 32, 4, 128], P(None, 'row'), may hold values from -6 to 6
- span_offsets: int32 [2, 32], P(None, 'row'), may hold values from 0 to 12543, as said below
- panels: bfloat16 [2, 256, 50176], P(None, 'col', 'row'), may hold values from -0.026785714 to 0.026785714
Outputs:
- back_vectors: float32 [1024, 50176], P('col', 'row')
Inputs may be any that keep to these rules, and one draw needn't show every extreme that they name: `span_offsets`: each block starts within the rows of its index of row and ends at most 128 rows after them, and inside the matrix; on every index of row but the last the last block of each sweep reaches into the next index's rows.
All inputs are finite; a program needn't handle non-finite values.
Results may differ from a plain program's by a relative error of at most 0.0075.
Values may be sent and summed in bfloat16 or wider, within the bound.
A program may use at most 128 MiB of HBM per device.

v0:
```python
import jax
import jax.numpy as jnp
from jax import lax
from jax.sharding import PartitionSpec as P

PRECISE = lax.Precision.HIGHEST
CONTRACT_LAST = (((1,), (1,)), ((), ()))
CONTRACT_FIRST = (((0,), (0,)), ((), ()))


def from_behind(value, axis, steps):
    count = lax.axis_size(axis)
    first, last = (max(0, -steps), min(count, count - steps))
    return lax.ppermute(value, axis, [(source, source + steps) for source in range(first, last)])


def wy_matrix(gram_mat):
    return jnp.triu(gram_mat, 1) + 0.5 * jnp.diag(jnp.diag(gram_mat))


def upper_solve(matrix, right):
    order = matrix.shape[0]
    if order <= 8:
        solved = [None] * order
        for back_at in range(order - 1, -1, -1):
            value = right[back_at]
            for later in range(back_at + 1, order):
                value = value - matrix[back_at, later] * solved[later]
            solved[back_at] = value / matrix[back_at, back_at]
        return jnp.stack(solved, axis=0)

    def step(count, solution):
        place = (order - 1 - count).astype(jnp.int32)
        matrow = lax.dynamic_index_in_dim(matrix, place, 0, keepdims=False)
        rhsrow = lax.dynamic_index_in_dim(right, place, 0, keepdims=False)
        pivot = lax.dynamic_index_in_dim(matrow, place, 0, keepdims=False)
        partial_sum = jnp.dot(matrow, solution, precision=PRECISE)
        value = (rhsrow - partial_sum) / pivot
        return lax.dynamic_update_index_in_dim(solution, value, place, 0)

    return lax.fori_loop(0, order, step, jnp.zeros(right.shape, jnp.float32))


def apply_span(window, vectors):
    gram_mat = jnp.dot(vectors, vectors.T, precision=PRECISE)
    inner = jnp.dot(vectors, window.T, precision=PRECISE)
    coeffs = upper_solve(wy_matrix(gram_mat), inner)
    return window - jnp.dot(coeffs.T, vectors, precision=PRECISE)


def run_spans(block, vectors, offsets, band_len):

    def advance(span_at, state):
        begin_at = offsets[span_at]
        window = lax.dynamic_slice_in_dim(state, begin_at, band_len, 1)
        return lax.dynamic_update_slice_in_dim(
            state, apply_span(window, vectors[span_at]), begin_at, 1
        )

    return lax.fori_loop(0, vectors.shape[0], advance, block)


def sweep_chain(eigen, vectors, offsets, band_len):
    columns, rows_dev = eigen.shape
    row_count = lax.axis_size("row")
    row_index = lax.axis_index("row")
    below = from_behind(eigen[:, :band_len], "row", -1)
    extended = jnp.concatenate([eigen, below], axis=1)

    def section(moment, state):
        finished = lax.cond(
            row_index == moment,
            lambda inside: run_spans(inside, vectors, offsets, band_len),
            lambda inside: inside,
            state,
        )
        arrived = from_behind(finished[:, rows_dev:], "row", 1)
        replaced = lax.dynamic_update_slice_in_dim(finished, arrived, 0, 1)
        return jnp.where(row_index == moment + 1, replaced, finished)

    extended = lax.fori_loop(0, row_count, section, extended)
    return extended[:, :rows_dev]


def panel_update(eigen, reflect, gram_mat, inner):
    coeffs = upper_solve(wy_matrix(gram_mat), inner)
    return eigen - lax.dot_general(
        coeffs.astype(jnp.bfloat16), reflect, CONTRACT_FIRST, preferred_element_type=jnp.float32
    )


def local_sums(reflect, eigen):
    gram_mat = lax.dot_general(reflect, reflect, CONTRACT_LAST, preferred_element_type=jnp.float32)
    inner = lax.dot_general(
        reflect, eigen.astype(jnp.bfloat16), CONTRACT_LAST, preferred_element_type=jnp.float32
    )
    return (gram_mat, inner)


def local(eigvecs, span_vectors, span_offsets, panels):
    band_len = span_vectors.shape[3]
    eigen = eigvecs
    for sweep_at in range(span_vectors.shape[0]):
        eigen = sweep_chain(eigen, span_vectors[sweep_at], span_offsets[sweep_at], band_len)
    gathered = lax.all_gather(panels, "col", axis=1, tiled=True)
    for panel_at in range(gathered.shape[0]):
        reflect = gathered[panel_at]
        gram_mat, inner = local_sums(reflect, eigen)
        gram_mat, inner = (
            lax.psum(gram_mat.astype(jnp.bfloat16), "row").astype(jnp.float32),
            lax.psum(inner.astype(jnp.bfloat16), "row").astype(jnp.float32),
        )
        eigen = panel_update(eigen, reflect, gram_mat, inner)
    return eigen


def solution(mesh):
    return jax.shard_map(
        local,
        mesh=mesh,
        in_specs=(
            P("col", "row"),
            P(None, "row", None, None),
            P(None, "row"),
            P(None, "col", "row"),
        ),
        out_specs=P("col", "row"),
        check_vma=False,
    )
```

profile of v0, /device:TPU:0, one launch (start us, length us, event | category | flops | bytes accessed | tf_op | source)
XLA Modules:
  0.0 1732.4 jit_solution(11646775154320812110)
XLA Ops:
  17.2 368.3 %while.90 = (s32[]{:T(128)}, f32[128,12672]{1,0:T(8,128)}, s32[]{:T(128)}, s32[8]{0:T(128)S(1)}, f32[8,4,128]{2,1,0:T(4,128)S(1)}, /*index=5*/s32[]{:T(128)}) while((s32[]{:T(128)}, f32[128,12672]{1,0:T(8,128)}, s32[]{:T(128)}, s32[8]{0:T(128)S(1)}, f32[8,4,128]{2,1,0:T(4,128)S(1)}, /*index=5*/s32[]{:T(128)}) %tuple.227), condition=%wide.region_5.6_spmd, body=%wide.region_0.5_spmd.sunk | while | flops 1633914 | bytes 933132 | solution.py:81
  17.2 114.9 %conditional.4 = (f32[128,12672]{1,0:T(8,128)}) conditional(s32[]{:T(128)} %convert_element_type.98, f32[128,12672]{1,0:T(8,128)} %get-tuple-element.998, (s32[8]{0:T(128)S(1)}, f32[8,4,128]{2,1,0:T(4,128)S(1)}, f32[128,12672]{1,0:T(8,128)}) %tuple.210), branch_computations={%region_1.0_spmd, %region_2.4_spmd} | conditional | flops 1617525 | bytes 343151 | solution.py:71
  17.2 114.9 %while.88 = (s32[]{:T(128)}, f32[128,12672]{1,0:T(8,128)}, s32[8]{0:T(128)S(1)}, f32[8,4,128]{2,1,0:T(4,128)S(1)}, s32[]{:T(128)}, /*index=5*/s32[]{:T(128)}, s32[]{:T(128)}) while((s32[]{:T(128)}, f32[128,12672]{1,0:T(8,128)}, s32[8]{0:T(128)S(1)}, f32[8,4,128]{2,1,0:T(4,128)S(1)}, s32[]{:T(128)}, /*index=5*/s32[]{:T(128)}, s32[]{:T(128)}) %tuple.224), condition=%wide.region_4.3_spmd, body=%wide.region_3.2_spmd.sunk | while | flops 1617525 | bytes 343079 | solution.py:60
  36.8 6.2 subtract_divide_fusion.13
  51.2 6.2 subtract_divide_fusion.13
  65.6 6.2 subtract_divide_fusion.13
  79.9 6.2 subtract_divide_fusion.13
  94.3 6.2 subtract_divide_fusion.13
  137.5 117.2 %collective-permute-start.1 = (f32[128,128]{1,0:T(8,128)S(1)}, f32[128,128]{1,0:T(8,128)S(1)}, u32[]{:S(2)}, u32[]{:S(2)}) collective-permute-start(f32[128,128]{1,0:T(8,128)S(1)} %slice.358), channel_id=1, source_target_pairs={{0,8},{8,16},{16,24},{1,9},{9,17},{17,25},{2,10},{10,18},{18,26},{... | collective-permute-start | bytes 196616 | tf_op jit(solution)/shard_map/while/body/eval_jaxpr/ppermute | solution.py:14
  263.6 119.6 %collective-permute-start.1 = (f32[128,128]{1,0:T(8,128)S(1)}, f32[128,128]{1,0:T(8,128)S(1)}, u32[]{:S(2)}, u32[]{:S(2)}) collective-permute-start(f32[128,128]{1,0:T(8,128)S(1)} %slice.358), channel_id=1, source_target_pairs={{0,8},{8,16},{16,24},{1,9},{9,17},{17,25},{2,10},{10,18},{18,26},{... | collective-permute-start | bytes 196616 | tf_op jit(solution)/shard_map/while/body/eval_jaxpr/ppermute | solution.py:14
  394.9 7.2 fusion.60
  402.1 368.6 %while.91 = (s32[]{:T(128)}, f32[128,12672]{1,0:T(8,128)}, s32[]{:T(128)}, s32[8]{0:T(128)S(1)}, f32[8,4,128]{2,1,0:T(4,128)S(1)}, /*index=5*/s32[]{:T(128)}) while((s32[]{:T(128)}, f32[128,12672]{1,0:T(8,128)}, s32[]{:T(128)}, s32[8]{0:T(128)S(1)}, f32[8,4,128]{2,1,0:T(4,128)S(1)}, /*index=5*/s32[]{:T(128)}) %tuple.230), condition=%wide.region_11.12_spmd, body=%wide.region_6.11_spmd.sunk | while | flops 1633914 | bytes 933132 | solution.py:81
  402.1 114.9 %conditional.5 = (f32[128,12672]{1,0:T(8,128)}) conditional(s32[]{:T(128)} %convert_element_type.99, f32[128,12672]{1,0:T(8,128)} %get-tuple-element.1016, (s32[8]{0:T(128)S(1)}, f32[8,4,128]{2,1,0:T(4,128)S(1)}, f32[128,12672]{1,0:T(8,128)}) %tuple.212), branch_computations={%region_7.7_spmd, %region_8.10_spmd} | conditional | flops 1617525 | bytes 343151 | solution.py:71
  402.1 114.9 %while.89 = (s32[]{:T(128)}, f32[128,12672]{1,0:T(8,128)}, s32[8]{0:T(128)S(1)}, f32[8,4,128]{2,1,0:T(4,128)S(1)}, s32[]{:T(128)}, /*index=5*/s32[]{:T(128)}, s32[]{:T(128)}) while((s32[]{:T(128)}, f32[128,12672]{1,0:T(8,128)}, s32[8]{0:T(128)S(1)}, f32[8,4,128]{2,1,0:T(4,128)S(1)}, s32[]{:T(128)}, /*index=5*/s32[]{:T(128)}, s32[]{:T(128)}) %tuple.221), condition=%wide.region_10.9_spmd, body=%wide.region_9.8_spmd.sunk | while | flops 1617525 | bytes 343079 | solution.py:60
  479.2 6.2 subtract_divide_fusion.12
  522.4 117.4 %collective-permute-start = (f32[128,128]{1,0:T(8,128)S(1)}, f32[128,128]{1,0:T(8,128)S(1)}, u32[]{:S(2)}, u32[]{:S(2)}) collective-permute-start(f32[128,128]{1,0:T(8,128)S(1)} %slice.359), channel_id=1, source_target_pairs={{0,8},{8,16},{16,24},{1,9},{9,17},{17,25},{2,10},{10,18},{18,26},{... | collective-permute-start | bytes 196616 | tf_op jit(solution)/shard_map/while/body/eval_jaxpr/ppermute | solution.py:14
  648.6 119.6 %collective-permute-start = (f32[128,128]{1,0:T(8,128)S(1)}, f32[128,128]{1,0:T(8,128)S(1)}, u32[]{:S(2)}, u32[]{:S(2)}) collective-permute-start(f32[128,128]{1,0:T(8,128)S(1)} %slice.359), channel_id=1, source_target_pairs={{0,8},{8,16},{16,24},{1,9},{9,17},{17,25},{2,10},{10,18},{18,26},{... | collective-permute-start | bytes 196616 | tf_op jit(solution)/shard_map/while/body/eval_jaxpr/ppermute | solution.py:14
  770.7 7.1 fusion.65
  778.0 7.2 fusion.59
  785.2 140.6 %all-reduce.7.cloned.1.call-done = (bf16[256,128]{1,0:T(8,128)(2,1)}, bf16[256,256]{1,0:T(8,128)(2,1)}) async-done(((bf16[256,128]{1,0:T(8,128)(2,1)}, bf16[256,256]{1,0:T(8,128)(2,1)}), (bf16[256,128]{1,0:T(8,128)(2,1)}, bf16[256,256]{1,0:T(8,128)(2,1)})) %all-reduce.7.cloned.1.call-update) | async-done | bytes 196624 | tf_op jit(solution)/shard_map/psum | solution.py:111
  930.9 376.1 %while.92 = (s32[]{:T(128)}, f32[256,128]{1,0:T(8,128)S(1)}, f32[256,128]{1,0:T(8,128)S(1)}, f32[256,256]{1,0:T(8,128)S(1)}, s32[]{:T(128)}, /*index=5*/s32[]{:T(128)}, s32[]{:T(128)}, s32[]{:T(128)}) while((s32[]{:T(128)}, f32[256,128]{1,0:T(8,128)S(1)}, f32[256,128]{1,0:T(8,128)S(1)}, f32[256,256]{1,0:T(8,128)S(1)}, s32[]{:T(128)}, ...), condition=%wide.region_15.16_spmd, body=%wide.region_14.15_spmd.sunk | while | flops 393479 | bytes 135335 | solution.py:41
  1321.0 32.2 %all-reduce.5.cloned.1.call-done = (bf16[256,128]{1,0:T(8,128)(2,1)}, bf16[256,256]{1,0:T(8,128)(2,1)}) async-done(((bf16[256,128]{1,0:T(8,128)(2,1)}, bf16[256,256]{1,0:T(8,128)(2,1)}), (bf16[256,128]{1,0:T(8,128)(2,1)}, bf16[256,256]{1,0:T(8,128)(2,1)})) %all-reduce.5.cloned.1.call-update) | async-done | bytes 196624 | tf_op jit(solution)/shard_map/psum | solution.py:111
  1358.4 358.8 %while.93 = (s32[]{:T(128)}, f32[256,128]{1,0:T(8,128)S(1)}, f32[256,128]{1,0:T(8,128)S(1)}, f32[256,256]{1,0:T(8,128)S(1)}, s32[]{:T(128)}, /*index=5*/s32[]{:T(128)}, s32[]{:T(128)}, s32[]{:T(128)}) while((s32[]{:T(128)}, f32[256,128]{1,0:T(8,128)S(1)}, f32[256,128]{1,0:T(8,128)S(1)}, f32[256,256]{1,0:T(8,128)S(1)}, s32[]{:T(128)}, ...), condition=%wide.region_19.20_spmd, body=%wide.region_18.19_spmd.sunk | while | flops 393479 | bytes 135335 | solution.py:41
  1717.2 8.7 convolution_subtract_fusion.2
  (1757 shorter events, 960.7 us)
Async XLA Ops:
  6.5 388.3 %all-gather.2.cloned.1.call-start = ((), (), s32[]{:S(2)}) async-start(), calls=%async_computation | async-start | bytes 14450688 | tf_op jit(solution)/shard_map/all_gather | solution.py:105
  7.3 918.5 %all-reduce.7.cloned.1.call-start = ((), (), s32[]{:S(2)}) async-start(), calls=%async_computation.2 | async-start | bytes 393216 | tf_op jit(solution)/shard_map/psum | solution.py:111
  8.1 3.1 collective-permute-start.2
  133.0 2.2 collective-permute-start.1
  137.5 118.1 %collective-permute-start.1 = (f32[128,128]{1,0:T(8,128)S(1)}, f32[128,128]{1,0:T(8,128)S(1)}, u32[]{:S(2)}, u32[]{:S(2)}) collective-permute-start(f32[128,128]{1,0:T(8,128)S(1)} %slice.358), channel_id=1, source_target_pairs={{0,8},{8,16},{16,24},{1,9},{9,17},{17,25},{2,10},{10,18},{18,26},{... | collective-permute-start | bytes 196616 | tf_op jit(solution)/shard_map/while/body/eval_jaxpr/ppermute | solution.py:14
  258.0 3.2 collective-permute-start.1
  263.6 120.4 %collective-permute-start.1 = (f32[128,128]{1,0:T(8,128)S(1)}, f32[128,128]{1,0:T(8,128)S(1)}, u32[]{:S(2)}, u32[]{:S(2)}) collective-permute-start(f32[128,128]{1,0:T(8,128)S(1)} %slice.358), channel_id=1, source_target_pairs={{0,8},{8,16},{16,24},{1,9},{9,17},{17,25},{2,10},{10,18},{18,26},{... | collective-permute-start | bytes 196616 | tf_op jit(solution)/shard_map/while/body/eval_jaxpr/ppermute | solution.py:14
  386.4 5.4 collective-permute-start.3
  517.8 2.2 collective-permute-start
  522.4 118.3 %collective-permute-start = (f32[128,128]{1,0:T(8,128)S(1)}, f32[128,128]{1,0:T(8,128)S(1)}, u32[]{:S(2)}, u32[]{:S(2)}) collective-permute-start(f32[128,128]{1,0:T(8,128)S(1)} %slice.359), channel_id=1, source_target_pairs={{0,8},{8,16},{16,24},{1,9},{9,17},{17,25},{2,10},{10,18},{18,26},{... | collective-permute-start | bytes 196616 | tf_op jit(solution)/shard_map/while/body/eval_jaxpr/ppermute | solution.py:14
  643.0 3.2 collective-permute-start
  648.6 120.5 %collective-permute-start = (f32[128,128]{1,0:T(8,128)S(1)}, f32[128,128]{1,0:T(8,128)S(1)}, u32[]{:S(2)}, u32[]{:S(2)}) collective-permute-start(f32[128,128]{1,0:T(8,128)S(1)} %slice.359), channel_id=1, source_target_pairs={{0,8},{8,16},{16,24},{1,9},{9,17},{17,25},{2,10},{10,18},{18,26},{... | collective-permute-start | bytes 196616 | tf_op jit(solution)/shard_map/while/body/eval_jaxpr/ppermute | solution.py:14
  777.8 575.4 %all-reduce.5.cloned.1.call-start = ((), (), s32[]{:S(2)}) async-start(), calls=%async_computation.1 | async-start | bytes 393216 | tf_op jit(solution)/shard_map/psum | solution.py:111
  1313.0 2.7 copy-start
Sparse Core Ops, SparseCore 0:
  9.5 182.0 all-gather.1
  777.9 147.8 all-reduce.6
  1321.1 32.0 all-reduce.4
where the time goes:
time: 1740 us; the launch traced here: 1730 us
  starting transfers between devices  484 us (28%)
  matrix products  480 us (28%)
  local copies, waits for them, and re-layouts  402 us (23%)
  waiting for transfers between devices  182 us (10%)
  other arithmetic  127 us (7%)
  loops' own time  44.8 us (3%)
    ppermute x10, starting transfers between devices, from_behind(): lax.ppermute(value, axis, [(source, source + steps) for source in range(f...  484 us
    dot_general x512, matrix products, step(): partial_sum = jnp.dot(matrow, solution, precision=PRECISE)  398 us
    dynamic_slice x512, local copies, waits for them, and re-layouts, step(): pivot = lax.dynamic_index_in_dim(matrow, place, 0, keepdims=False)  304 us
    psum x2, waiting for transfers between devices, local(): lax.psum(inner.astype(jnp.bfloat16), 'row').astype(jnp.float32)  173 us
    div x16, other arithmetic, upper_solve(): solved[back_at] = value / matrix[back_at, back_at]  98.5 us
  transfers between devices with their start and end apart: 13, of which 12 were waited for; matrix products, arithmetic and copies ran while one was open for 8% of the time, Pallas kernels for 0%

commit v1 on v0

v1 whole, which is shorter than its diff:
```python
import functools

import jax
import jax.numpy as jnp
from jax import lax
from jax.experimental import pallas as pl
from jax.experimental.pallas import tpu as pltpu
from jax.sharding import PartitionSpec as P

PRECISE = lax.Precision.HIGHEST
CONTRACT_LAST = (((1,), (1,)), ((), ()))
CONTRACT_FIRST = (((0,), (0,)), ((), ()))
LANES = 128


def shift_row(value, steps):
    count = lax.axis_size("row")
    first, last = (max(0, -steps), min(count, count - steps))
    return lax.ppermute(value, "row", [(source, source + steps) for source in range(first, last)])


def row_sum(value):
    count = lax.axis_size("row")
    if count & (count - 1):
        return lax.psum(value, "row")
    step = 1
    while step < count:
        value = value + lax.ppermute(value, "row", [(at, at ^ step) for at in range(count)])
        step *= 2
    return value


def spread_kernel(refl, offs_ref, vec_ref, out_ref):
    out_ref[...] = jnp.zeros_like(out_ref)
    spans = vec_ref.shape[0] // refl
    band = vec_ref.shape[1]
    wide = band + LANES
    per = 8 // refl
    for span_at in range(spans):
        group = span_at // per
        begin = offs_ref[span_at]
        base = pl.multiple_of(begin // LANES * LANES, LANES)
        rows = pl.ds(8 * group, 8)
        vectors = jnp.concatenate(
            [vec_ref[rows, :], jnp.zeros((8, LANES), jnp.float32)], axis=1
        )
        moved = pltpu.roll(vectors, begin - begin // LANES * LANES, 1)
        place = lax.broadcasted_iota(jnp.int32, (8, wide), 0) // refl
        out_ref[rows, pl.ds(base, wide)] += jnp.where(place == span_at % per, moved, 0.0)


def spread(vectors, offsets, refl, rows_dev):
    count, band = vectors.shape
    return pl.pallas_call(
        functools.partial(spread_kernel, refl),
        out_shape=jax.ShapeDtypeStruct((count, rows_dev + band), jnp.float32),
        in_specs=[
            pl.BlockSpec(memory_space=pltpu.SMEM),
            pl.BlockSpec(memory_space=pltpu.VMEM),
        ],
        out_specs=pl.BlockSpec(memory_space=pltpu.VMEM),
        cost_estimate=pl.CostEstimate(flops=0, bytes_accessed=8 * count * rows_dev, transcendentals=0),
    )(offsets, vectors)


def triangle_inverse(matrix):
    order = matrix.shape[0]
    row = lax.broadcasted_iota(jnp.int32, (order, order), 0)
    col = lax.broadcasted_iota(jnp.int32, (order, order), 1)
    diagonal = jnp.where(row == col, matrix, 0.0)
    down = 1.0 / jnp.sum(diagonal, axis=1, keepdims=True)
    across = 1.0 / jnp.sum(diagonal, axis=0, keepdims=True)
    inverse = jnp.where(row == col, down, 0.0)
    beside = (row // 2 == col // 2) & (row != col)
    inverse = inverse - jnp.where(beside, matrix * down * across, 0.0)
    size = 2
    while size < order:
        beside = (row // (2 * size) == col // (2 * size)) & (row // size != col // size)
        off = jnp.where(beside, matrix, 0.0)
        right = jnp.dot(off, inverse, precision=PRECISE, preferred_element_type=jnp.float32)
        inverse = inverse - jnp.dot(
            inverse, right, precision=PRECISE, preferred_element_type=jnp.float32
        )
        size *= 2
    return inverse


def solve_kernel(block, mat_ref, rhs_ref, out_ref):
    gram_mat = mat_ref[...]
    order = gram_mat.shape[0]
    row = lax.broadcasted_iota(jnp.int32, (order, order), 0)
    col = lax.broadcasted_iota(jnp.int32, (order, order), 1)
    before = (row // block > col // block) | ((row // block == col // block) & (row < col))
    matrix = jnp.where(before, gram_mat, jnp.where(row == col, 0.5 * gram_mat, 0.0))
    inverse = triangle_inverse(matrix)
    out_ref[...] = jnp.dot(
        inverse, rhs_ref[...], precision=PRECISE, preferred_element_type=jnp.float32
    ).astype(out_ref.dtype)


def solve(gram_mat, inner, block, dtype):
    order = gram_mat.shape[0]
    return pl.pallas_call(
        functools.partial(solve_kernel, block),
        out_shape=jax.ShapeDtypeStruct(inner.shape, dtype),
        in_specs=[pl.BlockSpec(memory_space=pltpu.VMEM)] * 2,
        out_specs=pl.BlockSpec(memory_space=pltpu.VMEM),
        cost_estimate=pl.CostEstimate(
            flops=200 * order**3, bytes_accessed=8 * order * order, transcendentals=0
        ),
    )(gram_mat, inner)


def sums_kernel(ref_ref, eig_ref, out_ref):
    width = ref_ref.shape[0]

    @pl.when(pl.program_id(0) == 0)
    def _():
        out_ref[...] = jnp.zeros_like(out_ref)

    reflect = ref_ref[...]
    out_ref[:, :width] += lax.dot_general(
        reflect, reflect, CONTRACT_LAST, preferred_element_type=jnp.float32
    )
    out_ref[:, width:] += lax.dot_general(
        reflect, eig_ref[...], CONTRACT_LAST, preferred_element_type=jnp.float32
    )


def tile_of(rows_dev, most):
    count = rows_dev // LANES
    return LANES * max(part for part in range(1, most + 1) if count % part == 0)


def local_sums(reflect, rounded):
    width, rows_dev = reflect.shape
    columns = rounded.shape[0]
    tile = tile_of(rows_dev, 14)
    return pl.pallas_call(
        sums_kernel,
        grid=(rows_dev // tile,),
        out_shape=jax.ShapeDtypeStruct((width, width + columns), jnp.float32),
        in_specs=[
            pl.BlockSpec((width, tile), lambda at: (0, at)),
            pl.BlockSpec((columns, tile), lambda at: (0, at)),
        ],
        out_specs=pl.BlockSpec((width, width + columns), lambda at: (0, 0)),
        cost_estimate=pl.CostEstimate(
            flops=2 * width * (width + columns) * rows_dev,
            bytes_accessed=2 * rows_dev * (width + columns),
            transcendentals=0,
        ),
    )(reflect, rounded)


def sweep_section(eigen, vectors, offsets):
    sweeps, spans_dev, refl, band = vectors.shape
    columns, rows_dev = eigen.shape
    rows = lax.axis_size("row")
    mine = lax.axis_index("row")
    own = spans_dev * refl
    count = sweeps * own
    spans = spread(vectors.reshape(count, band), offsets.reshape(-1), refl, rows_dev)
    tail = shift_row(spans[:, rows_dev:], 1)
    head = spans[:, :band]
    first = eigen[:, :band]
    inside = spans[:, :rows_dev]

    def times(left, right):
        return lax.dot_general(
            left, right, CONTRACT_LAST, precision=PRECISE, preferred_element_type=jnp.float32
        )

    packed = jnp.concatenate(
        [times(inside, eigen), times(tail, first), times(spans, spans), times(head, tail)], axis=1
    )
    packed = lax.all_gather(packed, "row", axis=0, tiled=False)
    inner = packed[:, :, :columns]
    above = packed[:, :, columns : 2 * columns]
    inner = inner + jnp.concatenate([above[1:], jnp.zeros_like(above[:1])], axis=0)
    shape = (rows, sweeps, own, sweeps, own)
    gram_own = packed[:, :, 2 * columns : 2 * columns + count].reshape(shape)
    gram_prev = packed[:, :, 2 * columns + count :].reshape(shape)
    same = jnp.eye(rows, dtype=jnp.float32)[:, :, None, None, None, None]
    back = jnp.eye(rows, k=-1, dtype=jnp.float32)[:, :, None, None, None, None]
    prev = gram_prev.transpose(0, 3, 4, 1, 2)
    full = same * gram_own[:, None] + back * gram_prev[:, None]
    full = full + back.transpose(1, 0, 2, 3, 4, 5) * prev[None]
    total = rows * count
    full = full.transpose(2, 0, 3, 4, 1, 5).reshape(total, total)
    inner = inner.reshape(rows, sweeps, own, columns).transpose(1, 0, 2, 3).reshape(total, columns)
    coeffs = solve(full, inner, refl, jnp.float32)
    coeffs = coeffs.reshape(sweeps, rows, own, columns)

    def of_row(place):
        return lax.dynamic_index_in_dim(coeffs, place, 1, keepdims=False).reshape(count, columns)

    own_part = of_row(mine)
    prev_part = of_row(jnp.maximum(mine - 1, 0))
    updated = eigen - lax.dot_general(
        own_part, inside, CONTRACT_FIRST, precision=PRECISE, preferred_element_type=jnp.float32
    )
    begin = updated[:, :band] - lax.dot_general(
        prev_part, tail, CONTRACT_FIRST, precision=PRECISE, preferred_element_type=jnp.float32
    )
    return lax.dynamic_update_slice_in_dim(updated, begin, 0, 1)


def local(eigvecs, span_vectors, span_offsets, panels):
    reflectors = [
        lax.all_gather(panels[panel_at], "col", axis=0, tiled=True)
        for panel_at in range(panels.shape[0])
    ]
    eigen = sweep_section(eigvecs, span_vectors, span_offsets)
    for reflect in reflectors:
        width = reflect.shape[0]
        both = row_sum(local_sums(reflect, eigen.astype(jnp.bfloat16)))
        coeffs = solve(both[:, :width], both[:, width:], width, jnp.bfloat16)
        eigen = eigen - lax.dot_general(
            coeffs, reflect, CONTRACT_FIRST, preferred_element_type=jnp.float32
        )
    return eigen


def solution(mesh):
    return jax.shard_map(
        local,
        mesh=mesh,
        in_specs=(
            P("col", "row"),
            P(None, "row", None, None),
            P(None, "row"),
            P(None, "col", "row"),
        ),
        out_specs=P("col", "row"),
        check_vma=False,
    )
```

time: 1740 us -> 264 us (0.15)
  starting transfers between devices: 484 us -> 5.65 us
  matrix products: 480 us -> 42.5 us
  local copies, waits for them, and re-layouts: 402 us -> 19.6 us
  other arithmetic: 127 us -> 7.69 us
  waiting for transfers between devices: 182 us -> 117 us
  Pallas kernels: 0 us -> 48.8 us
  loops' own time: 44.8 us -> 0 us
    ppermute x10 -> x5, starting transfers between devices: 484 us -> 5.61 us  [the longest x4 3.09 us: row_sum(): lax.ppermute(value, 'row', [(at, at ^ step) for at in range(count)])]
    dot_general x566 -> x8, matrix products: 480 us -> 42.5 us  [the longest x2 18.5 us: local(): lax.dot_general(coeffs, reflect, CONTRACT_FIRST, preferred_element_type=j...]
    dynamic_slice x528 -> x1, local copies, waits for them, and re-layouts: 313 us -> 0.84 us  [of_row(): lax.dynamic_index_in_dim(coeffs, place, 1, keepdims=False)]
    psum x2 -> x0, waiting for transfers between devices: 173 us -> none  [local(): lax.psum(inner.astype(jnp.bfloat16), 'row').astype(jnp.float32)]
    div x16 -> x0, other arithmetic: 98.5 us -> none  [upper_solve(): solved[back_at] = value / matrix[back_at, back_at]]
    all_gather x1 -> x2, waiting for transfers between devices: 0.01 us -> 92.9 us  [local(): lax.all_gather(panels[panel_at], 'col', axis=0, tiled=True)]
    pallas_call x0 -> x6, Pallas kernels: none -> 48.8 us  [the longest x3 28.6 us: solve(): pl.pallas_call(functools.partial(solve_kernel, block), out_shape=jax.Shap...]
    dynamic_update_slice x528 -> x0, local copies, waits for them, and re-layouts: 47.2 us -> none  [the longest x16 27.7 us: advance(): lax.dynamic_update_slice_in_dim(state, apply_span(window, vectors[span_at...]
  transfers between devices with their start and end apart: 13 -> 7, of which waited for: 12 -> 6; matrix products, arithmetic and copies ran while one was open for 8% -> 20% of each run, Pallas kernels for 0% -> 12%
where the time goes in v1:
time: 264 us; the launch traced here: 263 us
  waiting for transfers between devices  117 us (44%)
  Pallas kernels  48.8 us (18%)
  matrix products  42.5 us (16%)
  local copies, waits for them, and re-layouts  19.6 us (7%)
  between operations  13.5 us (5%)
  blocking collectives  8.09 us (3%)
  other arithmetic  7.69 us (3%)
  starting transfers between devices  5.65 us (2%)
    all_gather x2, waiting for transfers between devices, local(): lax.all_gather(panels[panel_at], 'col', axis=0, tiled=True)  92.9 us
    pallas_call x3, Pallas kernels, solve(): pl.pallas_call(functools.partial(solve_kernel, block), out_shape=jax.Shap...  28.6 us
    ppermute x4, waiting for transfers between devices, row_sum(): lax.ppermute(value, 'row', [(at, at ^ step) for at in range(count)])  23.2 us
    dot_general x2, matrix products, local(): lax.dot_general(coeffs, reflect, CONTRACT_FIRST, preferred_element_type=j...  18.5 us
    pallas_call x2, Pallas kernels, local_sums(): pl.pallas_call(sums_kernel, grid=(rows_dev // tile,), out_shape=jax.Shape...  17.5 us
    dot_general x4, matrix products, times(): lax.dot_general(left, right, CONTRACT_LAST, precision=PRECISE, preferred_...  16.1 us
    all_gather x1, blocking collectives, sweep_section(): packed = lax.all_gather(packed, 'row', axis=0, tiled=False)  8.09 us
    dot_general x1, matrix products, sweep_section(): lax.dot_general(own_part, inside, CONTRACT_FIRST, precision=PRECISE, pref...  7.66 us
  transfers between devices with their start and end apart: 7, of which 6 were waited for; matrix products, arithmetic and copies ran while one was open for 20% of the time, Pallas kernels for 12%

profile of v1, /device:TPU:0, one launch (start us, length us, event | category | flops | bytes accessed | tf_op | source)
XLA Modules:
  0.0 262.7 jit_solution(15327719398159313659)
XLA Ops:
  6.5 2.6 %fusion.12 = (bf16[1,32,12544]{2,1,0:T(8,128)(2,1)}, bf16[1,32,12544]{2,1,0:T(8,128)(2,1)}) fusion(bf16[2,32,12544]{2,1,0:T(8,128)(2,1)} %param.7), kind=kLoop, calls=%fused_computation.26 | loop fusion | bytes 3211264 | tf_op jit(solution)/shard_map/slice | solution.py:211
  11.3 2.8 %shard_map.46 = f32[64,12672]{1,0:T(8,128)} custom-call(s32[16]{0:T(128)} %reshape.85.offs_ref, f32[64,128]{1,0:T(8,128)} %bitcast.50), custom_call_target="tpu_custom_call" | custom-call | bytes 6422528 | tf_op jit(solution)/shard_map/pallas_call | solution.py:54
  15.0 2.5 collective-permute-start
  17.6 6.3 %fusion.15 = f32[64,64]{1,0:T(8,128)S(1)} fusion(f32[64,12672]{1,0:T(8,128)} %shard_map.46), kind=kOutput, calls=%fused_computation.29 | convolution fusion | flops 622854144 | bytes 3260416 | tf_op jit(solution)/shard_map/dot_general | solution.py:170
  23.9 8.5 %fusion.1 = f32[64,128]{1,0:T(8,128)S(1)} fusion(f32[128,12544]{1,0:T(8,128)} %param.4, f32[64,12672]{1,0:T(8,128)S(1)} %copy-done), kind=kOutput, calls=%fused_computation.4 | convolution fusion | flops 1233125376 | bytes 9666560 | tf_op jit(solution)/shard_map/dot_general | solution.py:170
  33.8 8.1 %all-gather = f32[256,384]{1,0:T(8,128)S(1)} all-gather(f32[64,384]{1,0:T(8,128)S(1)} %pad_maximum_fusion), channel_id=2, replica_groups=mesh['row'=4,'col'=8] {'row'}, dimensions={0}, use_global_device_ids=true | all-gather | bytes 491520 | tf_op jit(solution)/shard_map/all_gather | solution.py:177
  47.0 2.4 multiply_add_fusion
  49.4 2.6 add.46.mat_ref
  53.7 9.5 %shard_map.47 = f32[256,128]{1,0:T(8,128)} custom-call(f32[256,256]{1,0:T(8,128)} %add.46.mat_ref, f32[256,128]{1,0:T(8,128)} %bitcast.48), custom_call_target="tpu_custom_call" | custom-call | flops 3355443200 | bytes 524288 | tf_op jit(solution)/shard_map/pallas_call | solution.py:103
  64.0 7.7 %convolution_subtract_fusion.2 = f32[128,12544]{1,0:T(8,128)S(1)} fusion(f32[128,12544]{1,0:T(8,128)} %param.4, f32[64,128]{1,0:T(8,128)S(1)} %bitcast.47, f32[64,12672]{1,0:T(8,128)S(1)} %copy-done), kind=kOutput, calls=%fused_computation.2 | convolution fusion | flops 1234731008 | bytes 16089088 | tf_op jit(solution)/shard_map/dot_general | solution.py:200
  72.0 2.7 %copy-done.1 = f32[128,12544]{1,0:T(8,128)} copy-done((f32[128,12544]{1,0:T(8,128)}, f32[128,12544]{1,0:T(8,128)S(1)}, u32[]{:S(2)}) %copy-start.1) | copy-done | bytes 6422552
  74.8 2.0 convert_element_type.26.eig_ref
  76.7 35.8 %all-gather.6.cloned.1.call-done = bf16[1,256,12544]{2,1,0:T(8,128)(2,1)} async-done(((bf16[1,32,12544]{2,1,0:T(8,128)(2,1)}), bf16[1,256,12544]{2,1,0:T(8,128)(2,1)}) %all-gather.6.cloned.1.call-update) | async-done | bytes 6422544 | tf_op jit(solution)/shard_map/all_gather | solution.py:211
  112.6 8.7 %shard_map.48 = f32[256,384]{1,0:T(8,128)} custom-call(bf16[256,12544]{1,0:T(8,128)(2,1)} %bitcast.41, bf16[128,12544]{1,0:T(8,128)(2,1)} %convert_element_type.26.eig_ref), custom_call_target="tpu_custom_call" | custom-call | flops 2466250752 | bytes 9633792 | tf_op jit(solution)/shard_map/pallas_call | solution.py:139
  121.3 1.9 collective-permute-done.1
  125.8 9.7 %collective-permute-done.2 = f32[256,384]{1,0:T(8,128)S(1)} collective-permute-done((f32[256,384]{1,0:T(8,128)S(1)}, f32[256,384]{1,0:T(8,128)S(1)}, u32[]{:S(2)}, u32[]{:S(2)}) %collective-permute-start.2) | collective-permute-done | bytes 393248 | tf_op jit(solution)/shard_map/ppermute | solution.py:28
  136.9 9.5 %shard_map.49 = bf16[256,128]{1,0:T(8,128)(2,1)} custom-call(f32[256,256]{1,0:T(8,128)} %slice.70.mat_ref, f32[256,128]{1,0:T(8,128)} %slice.71.rhs_ref), custom_call_target="tpu_custom_call" | custom-call | flops 3355443200 | bytes 524288 | tf_op jit(solution)/shard_map/pallas_call | solution.py:103
  146.5 9.7 %fusion.14 = (bf16[128,12544]{1,0:T(8,128)(2,1)}, f32[128,12544]{1,0:T(8,128)}) fusion(f32[128,12544]{1,0:T(8,128)} %copy-done.1, bf16[256,128]{1,0:T(8,128)(2,1)} %shard_map.49, bf16[1,256,12544]{2,1,0:T(8,128)(2,1)} %all-gather.6.cloned.1.call-done), kind=kOutput, calls=%fused_computation.28 | convolution fusion | flops 825294848 | bytes 22544384 | tf_op jit(solution)/shard_map/dot_general | solution.py:219
  156.2 57.0 %all-gather.8.cloned.1.call-done = bf16[1,256,12544]{2,1,0:T(8,128)(2,1)} async-done(((bf16[1,32,12544]{2,1,0:T(8,128)(2,1)}), bf16[1,256,12544]{2,1,0:T(8,128)(2,1)}) %all-gather.8.cloned.1.call-update) | async-done | bytes 6422544 | tf_op jit(solution)/shard_map/all_gather | solution.py:211
  213.2 8.7 %shard_map.50 = f32[256,384]{1,0:T(8,128)} custom-call(bf16[256,12544]{1,0:T(8,128)(2,1)} %bitcast.40, bf16[128,12544]{1,0:T(8,128)(2,1)} %get-tuple-element.11.eig_ref), custom_call_target="tpu_custom_call" | custom-call | flops 2466250752 | bytes 9633792 | tf_op jit(solution)/shard_map/pallas_call | solution.py:139
  222.0 1.9 collective-permute-done.3
  226.5 9.7 %collective-permute-done.4 = f32[256,384]{1,0:T(8,128)S(1)} collective-permute-done((f32[256,384]{1,0:T(8,128)S(1)}, f32[256,384]{1,0:T(8,128)S(1)}, u32[]{:S(2)}, u32[]{:S(2)}) %collective-permute-start.4) | collective-permute-done | bytes 393248 | tf_op jit(solution)/shard_map/ppermute | solution.py:28
  237.6 9.5 %shard_map.51 = bf16[256,128]{1,0:T(8,128)(2,1)} custom-call(f32[256,256]{1,0:T(8,128)} %slice.72.mat_ref, f32[256,128]{1,0:T(8,128)} %slice.73.rhs_ref), custom_call_target="tpu_custom_call" | custom-call | flops 3355443200 | bytes 524288 | tf_op jit(solution)/shard_map/pallas_call | solution.py:103
  247.1 8.7 %convolution_subtract_fusion = f32[128,12544]{1,0:T(8,128)} fusion(f32[128,12544]{1,0:T(8,128)} %get-tuple-element.12, bf16[256,128]{1,0:T(8,128)(2,1)} %shard_map.51, bf16[1,256,12544]{2,1,0:T(8,128)(2,1)} %all-gather.8.cloned.1.call-done), kind=kOutput, calls=%fused_computation | convolution fusion | flops 823689216 | bytes 19333120 | tf_op jit(solution)/shard_map/dot_general | solution.py:219
  (39 shorter events, 20.4 us)
Async XLA Ops:
  6.5 106.0 %all-gather.6.cloned.1.call-start = ((), (), s32[]{:S(2)}) async-start(), calls=%async_computation | async-start | bytes 7225344 | tf_op jit(solution)/shard_map/all_gather | solution.py:211
  9.2 204.0 %all-gather.8.cloned.1.call-start = ((), (), s32[]{:S(2)}) async-start(), calls=%async_computation.1 | async-start | bytes 7225344 | tf_op jit(solution)/shard_map/all_gather | solution.py:211
  14.0 9.9 %copy-start = (f32[64,12672]{1,0:T(8,128)S(1)}, f32[64,12672]{1,0:T(8,128)}, u32[]{:S(2)}) copy-start(f32[64,12672]{1,0:T(8,128)} %shard_map.46) | copy-start | bytes 9732100
  15.0 17.5 %collective-permute-start = (f32[64,128]{1,0:T(8,128)S(1)}, f32[64,128]{1,0:T(8,128)S(1)}, u32[]{:S(2)}, u32[]{:S(2)}) collective-permute-start(f32[64,128]{1,0:T(8,128)S(1)} %slice.63), channel_id=1, source_target_pairs={{0,8},{8,16},{16,24},{1,9},{9,17},{17,25},{2,10},{10,18},{18,26},{... | collective-permute-start | bytes 98312 | tf_op jit(solution)/shard_map/ppermute | solution.py:19
  41.9 1.4 copy-start.2
  72.0 2.7 %copy-start.1 = (f32[128,12544]{1,0:T(8,128)}, f32[128,12544]{1,0:T(8,128)S(1)}, u32[]{:S(2)}) copy-start(f32[128,12544]{1,0:T(8,128)S(1)} %fusion.3) | copy-start | bytes 19267588
  121.3 1.9 collective-permute-start.1
  124.3 11.2 %collective-permute-start.2 = (f32[256,384]{1,0:T(8,128)S(1)}, f32[256,384]{1,0:T(8,128)S(1)}, u32[]{:S(2)}, u32[]{:S(2)}) collective-permute-start(f32[256,384]{1,0:T(8,128)S(1)} %add.49), channel_id=1, source_target_pairs={{0,16},{8,24},{16,0},{24,8},{1,17},{9,25},{17,1},{25,9},{2,18},{10... | collective-permute-start | bytes 1179656 | tf_op jit(solution)/shard_map/ppermute | solution.py:28
  222.0 1.9 collective-permute-start.3
  225.0 11.2 %collective-permute-start.4 = (f32[256,384]{1,0:T(8,128)S(1)}, f32[256,384]{1,0:T(8,128)S(1)}, u32[]{:S(2)}, u32[]{:S(2)}) collective-permute-start(f32[256,384]{1,0:T(8,128)S(1)} %add.51), channel_id=1, source_target_pairs={{0,16},{8,24},{16,0},{24,8},{1,17},{9,25},{17,1},{25,9},{2,18},{10... | collective-permute-start | bytes 1179656 | tf_op jit(solution)/shard_map/ppermute | solution.py:28
Sparse Core Ops, SparseCore 0:
  9.5 102.9 all-gather.5
  114.7 98.4 all-gather.7
